TPU v7x, 32 devices: a whole 2x2x4 slice. The times are simulated.
32 devices in a mesh: ia: 4 (over y, x), ja: 4 (over z), col: 2 (over core).
Axes of the slice: x: 2, y: 2, z: 4, core: 2. Of those that a mesh axis runs over, the one named last changes fastest.
Arguments:
- pair_rep: bfloat16 [512, 512, 128], P('ia', 'ja'), may hold values from -6 to 6
- norm_gain: float32 [128], replicated, may hold values from 0.1 to 1.9
- weights: bfloat16 [4, 128, 128], P(None, None, 'col'), may hold values from -0.5 to 0.5
- residue_mask: int32 [512], replicated, may hold values 0 or 1
- product_grad: bfloat16 [512, 128, 512], P('ia', 'col', 'ja'), may hold values from -1 to 1
Outputs:
- pair_grad: bfloat16 [512, 512, 128], P('ia', 'ja')
- weight_grads: float32 [4, 128, 128], P(None, None, 'col')
All inputs are finite; a program needn't handle non-finite values.
Results may differ from a plain program's by a relative error of at most 0.0067.
Values may be sent and summed in bfloat16 or wider, within the bound.
A program may use at most 128 MiB of HBM per device.

v0:
```python
import jax
import jax.numpy as jnp
from jax import lax
from jax.sharding import PartitionSpec as P

CLIP_LIMIT = 64.0


def gate_terms(incoming, linear, gate_pre, pair_valid):
    sigmoid_gate = jax.nn.sigmoid(gate_pre)
    through = incoming * pair_valid
    return (through * sigmoid_gate, through * linear * sigmoid_gate * (1.0 - sigmoid_gate))


def on_device(pair_rep, norm_gain, weights, residue_mask, product_grad):
    row_count = pair_rep.shape[0]
    col_count = pair_rep.shape[1]
    row_first = lax.axis_index("ia") * row_count
    col_first = lax.axis_index("ja") * col_count
    validity = residue_mask.astype(jnp.float32)
    row_valid = lax.dynamic_slice_in_dim(validity, row_first, row_count)
    col_valid = lax.dynamic_slice_in_dim(validity, col_first, col_count)
    pair_valid = row_valid[:, None, None] * col_valid[None, None, :]
    floats = pair_rep.astype(jnp.float32)
    centred = floats - jnp.mean(floats, axis=-1, keepdims=True)
    inv_std = lax.rsqrt(jnp.mean(centred * centred, axis=-1, keepdims=True) + 1e-05)
    unit_rows = centred * inv_std
    normed = (unit_rows * norm_gain).astype(jnp.bfloat16)
    projected = jnp.einsum("ikd,wdc->wick", normed, weights, preferred_element_type=jnp.float32)
    left_side = (pair_valid * jax.nn.sigmoid(projected[1]) * projected[0]).astype(jnp.bfloat16)
    right_side = (pair_valid * jax.nn.sigmoid(projected[3]) * projected[2]).astype(jnp.bfloat16)
    row_panel = lax.all_gather(product_grad, "ja", axis=2, tiled=True)
    panel_part = row_panel
    grad_left = jnp.einsum(
        "icj,jck->ick",
        panel_part,
        lax.all_gather(right_side, "ia", axis=0, tiled=True),
        preferred_element_type=jnp.float32,
    )
    panel_part = row_panel
    grad_right = lax.psum_scatter(
        jnp.einsum("icj,ick->jck", panel_part, left_side, preferred_element_type=jnp.float32),
        "ia",
        scatter_dimension=0,
        tiled=True,
    )
    lin_a, gate_a = gate_terms(grad_left, projected[0], projected[1], pair_valid)
    lin_b, gate_b = gate_terms(grad_right, projected[2], projected[3], pair_valid)
    proj_grads = jnp.stack([lin_a, gate_a, lin_b, gate_b]).astype(jnp.bfloat16)
    grad_part = jnp.einsum("ikd,wick->wdc", normed, proj_grads, preferred_element_type=jnp.float32)
    input_part = jnp.einsum(
        "wick,wdc->ikd", proj_grads, weights, preferred_element_type=jnp.float32
    )
    normed_grad = lax.psum(input_part, "col")
    scaled = normed_grad * norm_gain
    pair_grad = inv_std * (
        scaled
        - jnp.mean(scaled, axis=-1, keepdims=True)
        - unit_rows * jnp.mean(scaled * unit_rows, axis=-1, keepdims=True)
    )
    summed = lax.psum(grad_part, ("ia", "ja"))
    squares = lax.psum(jnp.sum(summed * summed), "col")
    factor = jnp.minimum(1.0, CLIP_LIMIT * lax.rsqrt(squares + 1e-06))
    weight_grads = summed * factor
    return (pair_grad.astype(jnp.bfloat16), weight_grads)


def solution(mesh):
    placed = (P("ia", "ja", None), P(), P(None, None, "col"), P(), P("ia", "col", "ja"))
    return jax.shard_map(
        on_device,
        mesh=mesh,
        in_specs=placed,
        out_specs=(P("ia", "ja", None), P(None, None, "col")),
        check_vma=False,
    )
```

profile of v0, /device:TPU:0, one launch (start us, length us, event | category | flops | bytes accessed | tf_op | source)
XLA Modules:
  0.0 660.3 jit_solution(14896707460684824877)
XLA Ops:
  7.2 0.0 copy-start
  7.2 0.0 copy-start.10
  7.2 0.0 all-gather.5.cloned.1.call-start
  7.2 4.3 copy.18
  11.5 0.0 all-gather.5.cloned.1.call-update
  11.5 0.0 all-gather.3.cloned.1.call-start
  11.6 0.0 copy-done.10
  11.6 0.0 copy-start.2
  11.6 0.1 fusion.41
  11.7 0.1 broadcast_multiply_fusion.1
  11.8 0.0 copy-start.9
  11.8 3.5 convert_reduce_fusion
  15.3 0.0 copy-done.2
  15.3 4.8 fusion.10
  20.1 0.0 copy-done
  20.2 0.0 copy-done.9
  20.2 4.7 convolution_bitcast_fusion
  24.9 0.0 copy-start.1
  24.9 5.9 copy-done.1
  30.8 2.6 multiply_convert_fusion.5
  33.4 0.0 all-gather.3.cloned.1.call-update
  33.4 0.5 reduce-scatter.2.cloned.1.call-start
  33.9 129.6 %all-gather.5.cloned.1.call-done = bf16[128,64,512]{2,0,1:T(8,128)(2,1)} async-done(((bf16[128,64,128]{2,0,1:T(8,128)(2,1)}), bf16[128,64,512]{2,0,1:T(8,128)(2,1)}) %all-gather.5.cloned.1.call-update) | async-done | bytes 8388624 | tf_op jit(solution)/shard_map/all_gather | solution.py:32
  163.5 87.5 %all-gather.3.cloned.1.call-done = bf16[512,64,128]{2,1,0:T(8,128)(2,1)} async-done(((bf16[128,64,128]{2,1,0:T(8,128)(2,1)}), bf16[512,64,128]{2,1,0:T(8,128)(2,1)}) %all-gather.3.cloned.1.call-update) | async-done | bytes 8388624 | tf_op jit(solution)/shard_map/all_gather | solution.py:37
  251.0 25.2 %fusion.11 = f32[64,128,128]{2,1,0:T(8,128)} fusion(bf16[128,64,512]{2,0,1:T(8,128)(2,1)} %all-gather.5.cloned.1.call-done, bf16[512,64,128]{2,1,0:T(8,128)(2,1)} %all-gather.3.cloned.1.call-done), kind=kOutput, calls=%fused_computation.15 | convolution fusion | flops 1073741824 | bytes 20971520 | tf_op jit(solution)/shard_map/icj,jck->ick/dot_general | solution.py:34
  276.2 5.4 copy.20
  281.6 6.8 %fusion.28 = (bf16[1,128,64,128]{3,2,1,0:T(8,128)(2,1)S(1)}, bf16[1,128,64,128]{3,2,1,0:T(8,128)(2,1)}, bf16[128,64,128]{2,1,0:T(8,128)(2,1)S(1)}) fusion(f32[64,128,128]{1,0,2:T(8,128)} %copy.20, f32[128,128]{1,0:T(8,128)S(1)} %broadcast_multiply_fusion.1, f32[4,128,64,128]{3,2,0,1:T(8,128)} %copy-done.1), kind=kLoop, calls=%fused_computation.43 | loop fusion | flops 14680064 | bytes 18939904 | tf_op jit(solution)/shard_map/stack | solution.py:49
  288.5 14.1 %fusion.32 = f32[64,128,512]{2,1,0:T(8,128)} fusion(bf16[128,64,512]{2,0,1:T(8,128)(2,1)} %all-gather.5.cloned.1.call-done, bf16[128,64,128]{2,1,0:T(8,128)(2,1)S(1)} %get-tuple-element.8), kind=kOutput, calls=%fused_computation.47 | convolution fusion | flops 1073741824 | bytes 27262976 | tf_op jit(solution)/shard_map/icj,ick->jck/dot_general | solution.py:42
  302.6 16.6 %copy.23 = f32[64,128,512]{1,0,2:T(8,128)} copy(f32[64,128,512]{2,1,0:T(8,128)} %fusion.32) | data formatting | bytes 33554432 | tf_op jit(solution)/shard_map/icj,ick->jck/dot_general | solution.py:42
  319.2 0.0 reduce-scatter.2.cloned.1.call-update
  319.2 0.0 all-reduce.5.cloned.1.call-start
  319.2 153.8 %reduce-scatter.2.cloned.1.call-done = f32[128,64,128]{2,1,0:T(8,128)} async-done(((f32[512,64,128]{2,1,0:T(8,128)}), f32[128,64,128]{2,1,0:T(8,128)}) %reduce-scatter.2.cloned.1.call-update) | async-done | bytes 4194320 | tf_op jit(solution)/shard_map/reduce_scatter | solution.py:41
  473.1 6.0 fusion.30
  479.1 0.0 copy-start.7
  479.2 1.3 copy-done.7
  480.4 0.7 copy-done.8
  481.1 5.4 fusion.34
  486.5 0.0 all-reduce.5.cloned.1.call-update
  486.6 0.0 all-reduce.3.cloned.1.call-start
  486.6 6.5 convolution_bitcast_fusion.1
  493.1 0.0 all-reduce.3.cloned.1.call-update
  493.1 99.0 %all-reduce.5.cloned.1.call-done = f32[4,128,64]{1,2,0:T(8,128)} async-done(((f32[4,128,64]{1,2,0:T(8,128)}), f32[4,128,64]{1,2,0:T(8,128)}) %all-reduce.5.cloned.1.call-update) | async-done | bytes 131088 | tf_op jit(solution)/shard_map/psum | solution.py:61
  592.1 1.5 multiply_reduce_fusion.1
  593.7 3.1 psum.23
  597.4 1.6 broadcast_multiply_fusion
  599.0 32.2 %all-reduce.3.cloned.1.call-done = f32[128,128,128]{2,1,0:T(8,128)} async-done(((f32[128,128,128]{2,1,0:T(8,128)}), f32[128,128,128]{2,1,0:T(8,128)}) %all-reduce.3.cloned.1.call-update) | async-done | bytes 8388624 | tf_op jit(solution)/shard_map/psum | solution.py:54
  631.2 11.6 %multiply_reduce_fusion = (f32[128,128]{1,0:T(8,128)S(1)}, f32[128,128]{1,0:T(8,128)S(1)}) fusion(f32[128,128,128]{2,1,0:T(8,128)} %all-reduce.3.cloned.1.call-done, f32[128]{0:T(128)S(1)} %copy-done.9, f32[128,128]{1,0:T(8,128)S(1)} %add_rsqrt_fusion, f32[128,128]{1,0:T(8,128)S(1)} %broadcast_multiply_fusion.4, bf16[128,128,128]{2,1,0:T(8,128)(2,1)} %param.5), kind=kLoop, calls=%fused_computation.17 | loop fusion | flops 14647296 | bytes 12845568 | tf_op jit(solution)/shard_map/reduce_sum | solution.py:58
  642.8 10.7 %fusion.9 = bf16[128,128,128]{2,1,0:T(8,128)(2,1)} fusion(bf16[128,128,128]{2,1,0:T(8,128)(2,1)S(1)} %copy-done.4, f32[128,128,128]{2,1,0:T(8,128)S(1)} %copy-done.5, f32[128,128]{1,0:T(8,128)S(1)} %get-tuple-element.11, f32[128,128]{1,0:T(8,128)S(1)} %get-tuple-element.12, f32[128]{0:T(128)S(1)} %copy-done.9, f32[128,128]{1,0:T(8,128)S(1)} %add_rsqrt_fusion, ...), kind=kLoop, calls=%fused_computation.12 | loop fusion | flops 18874368 | bytes 17039872 | tf_op jit(solution)/shard_map/convert_element_type | solution.py:65
  (13 shorter events, 0.1 us)
Async XLA Ops:
  7.2 13.0 %copy-start = (bf16[4,128,64]{1,2,0:T(8,128)(2,1)S(1)}, bf16[4,128,64]{1,2,0:T(8,128)(2,1)}, u32[]{:S(2)}) copy-start(bf16[4,128,64]{1,2,0:T(8,128)(2,1)} %param.7) | copy-start | bytes 196612
  7.2 4.4 copy-start.10
  7.2 156.3 %all-gather.5.cloned.1.call-start = ((), (), s32[]{:S(2)}) async-start(), calls=%async_computation.2 | async-start | bytes 10485760 | tf_op jit(solution)/shard_map/all_gather | solution.py:32
  11.5 239.5 %all-gather.3.cloned.1.call-start = ((), (), s32[]{:S(2)}) async-start(), calls=%async_computation.1 | async-start | bytes 10485760 | tf_op jit(solution)/shard_map/all_gather | solution.py:37
  11.6 3.7 copy-start.2
  11.8 8.4 %copy-start.9 = (f32[128]{0:T(128)S(1)}, f32[128]{0:T(128)}, u32[]{:S(2)}) copy-start(f32[128]{0:T(128)} %param.6) | copy-start | bytes 1540
  24.9 5.9 copy-start.1
  33.4 439.6 %reduce-scatter.2.cloned.1.call-start = ((), (), s32[]{:S(2)}) async-start(), calls=%async_computation.3 | async-start | bytes 20971520 | tf_op jit(solution)/shard_map/reduce_scatter | solution.py:41
  319.2 272.9 %all-reduce.5.cloned.1.call-start = ((), (), s32[]{:S(2)}) async-start(), calls=%async_computation.5 | async-start | bytes 262144 | tf_op jit(solution)/shard_map/psum | solution.py:61
  473.1 8.0 %copy-start.3 = (bf16[128,128,128]{2,1,0:T(8,128)(2,1)S(1)}, bf16[128,128,128]{2,1,0:T(8,128)(2,1)}, u32[]{:S(2)}) copy-start(bf16[128,128,128]{2,1,0:T(8,128)(2,1)} %param.5) | copy-start | bytes 12582916
  473.1 8.0 %copy-start.6 = (bf16[1,128,64,128]{3,2,1,0:T(8,128)(2,1)S(1)}, bf16[1,128,64,128]{3,2,1,0:T(8,128)(2,1)}, u32[]{:S(2)}) copy-start(bf16[1,128,64,128]{3,2,1,0:T(8,128)(2,1)} %get-tuple-element.5) | copy-start | bytes 6291460
  479.1 1.3 copy-start.7
  479.1 2.0 copy-start.8
  486.6 144.6 %all-reduce.3.cloned.1.call-start = ((), (), s32[]{:S(2)}) async-start(), calls=%async_computation.4 | async-start | bytes 16777216 | tf_op jit(solution)/shard_map/psum | solution.py:54
  631.2 11.6 %copy-start.4 = (bf16[128,128,128]{2,1,0:T(8,128)(2,1)S(1)}, bf16[128,128,128]{2,1,0:T(8,128)(2,1)}, u32[]{:S(2)}) copy-start(bf16[128,128,128]{2,1,0:T(8,128)(2,1)} %param.5) | copy-start | bytes 12582916
  631.2 11.6 %copy-start.5 = (f32[128,128,128]{2,1,0:T(8,128)S(1)}, f32[128,128,128]{2,1,0:T(8,128)}, u32[]{:S(2)}) copy-start(f32[128,128,128]{2,1,0:T(8,128)} %all-reduce.3.cloned.1.call-done) | copy-start | bytes 25165828
Sparse Core Ops, SparseCore 0:
  11.6 151.8 all-gather.4
  165.4 85.6 all-gather.2
  319.3 153.7 reduce-scatter.1
  486.7 105.3 all-reduce.4
  594.4 36.6 all-reduce.2
where the time goes:
time: 668 us; the launch traced here: 660 us
  waiting for transfers between devices  502 us (75%)
  matrix products  55.9 us (8%)
  other arithmetic  49.3 us (7%)
  local copies, waits for them, and re-layouts  34.2 us (5%)
  between operations  14.9 us (2%)
    reduce_scatter x1, waiting for transfers between devices, on_device(): lax.psum_scatter(jnp.einsum('icj,ick->jck', panel_part, left_side, prefer...  154 us
    all_gather x1, waiting for transfers between devices, on_device(): row_panel = lax.all_gather(product_grad, 'ja', axis=2, tiled=True)  130 us
    psum x1, waiting for transfers between devices, on_device(): summed = lax.psum(grad_part, ('ia', 'ja'))  99 us
    all_gather x1, waiting for transfers between devices, on_device(): lax.all_gather(right_side, 'ia', axis=0, tiled=True)  87.5 us
    psum x1, waiting for transfers between devices, on_device(): normed_grad = lax.psum(input_part, 'col')  32.2 us
    dot_general x1, matrix products, on_device(): jnp.einsum('icj,jck->ick', panel_part, lax.all_gather(right_side, 'ia', a...  25.2 us
    dot_general x1, local copies, waits for them, and re-layouts, on_device(): jnp.einsum('icj,ick->jck', panel_part, left_side, preferred_element_type=...  16.6 us
    dot_general x1, matrix products, on_device(): jnp.einsum('icj,ick->jck', panel_part, left_side, preferred_element_type=...  14.1 us
  transfers between devices with their start and end apart: 5, of which 5 were waited for; matrix products, arithmetic and copies ran while one was open for 4% of the time, Pallas kernels for 0%

commit v1 on v0

--- a/solution.py
+++ b/solution.py
@@ -29,7 +29,12 @@
     projected = jnp.einsum("ikd,wdc->wick", normed, weights, preferred_element_type=jnp.float32)
     left_side = (pair_valid * jax.nn.sigmoid(projected[1]) * projected[0]).astype(jnp.bfloat16)
     right_side = (pair_valid * jax.nn.sigmoid(projected[3]) * projected[2]).astype(jnp.bfloat16)
-    row_panel = lax.all_gather(product_grad, "ja", axis=2, tiled=True)
+    ring = [product_grad]
+    for hop in range(3):
+        ring.append(lax.ppermute(ring[-1], "ja", [(dev, (dev + 1) % 4) for dev in range(4)]))
+    row_panel = jnp.roll(
+        jnp.concatenate(ring[::-1], axis=2), (lax.axis_index("ja") + 1) * ring[0].shape[2], axis=2
+    )
     panel_part = row_panel
     grad_left = jnp.einsum(
         "icj,jck->ick",

time: 668 us -> 619 us (0.927)
  waiting for transfers between devices: 502 us -> 427 us
  local copies, waits for them, and re-layouts: 34.2 us -> 54.9 us
    ppermute x0 -> x3, waiting for transfers between devices: none -> 144 us  [on_device(): lax.ppermute(ring[-1], 'ja', [(dev, (dev + 1) % 4) for dev in range(4)])]
    all_gather x1 -> x0, waiting for transfers between devices: 130 us -> none  [on_device(): row_panel = lax.all_gather(product_grad, 'ja', axis=2, tiled=True)]
    all_gather x1, waiting for transfers between devices: 87.5 us -> 0.01 us  [on_device(): lax.all_gather(right_side, 'ia', axis=0, tiled=True)]
    unnamed x23 -> x36, local copies, waits for them, and re-layouts: 12.2 us -> 29.9 us
  transfers between devices with their start and end apart: 5 -> 7, of which waited for: 5 -> 6; matrix products, arithmetic and copies ran while one was open for 4% -> 5% of each run, Pallas kernels for 0% -> 0%
where the time goes in v1:
time: 619 us; the launch traced here: 613 us
  waiting for transfers between devices  427 us (69%)
  matrix products  60 us (10%)
  local copies, waits for them, and re-layouts  54.9 us (9%)
  other arithmetic  49.6 us (8%)
  between operations  15 us (2%)
    reduce_scatter x1, waiting for transfers between devices, on_device(): lax.psum_scatter(jnp.einsum('icj,ick->jck', panel_part, left_side, prefer...  152 us
    ppermute x3, waiting for transfers between devices, on_device(): lax.ppermute(ring[-1], 'ja', [(dev, (dev + 1) % 4) for dev in range(4)])  144 us
    psum x1, waiting for transfers between devices, on_device(): summed = lax.psum(grad_part, ('ia', 'ja'))  98.9 us
    psum x1, waiting for transfers between devices, on_device(): normed_grad = lax.psum(input_part, 'col')  32.2 us
    unnamed x36, local copies, waits for them, and re-layouts  29.9 us
    dot_general x1, matrix products, on_device(): jnp.einsum('icj,jck->ick', panel_part, lax.all_gather(right_side, 'ia', a...  25.2 us
    dot_general x1, local copies, waits for them, and re-layouts, on_device(): jnp.einsum('icj,ick->jck', panel_part, left_side, preferred_element_type=...  16.6 us
    dot_general x1, matrix products, on_device(): jnp.einsum('icj,ick->jck', panel_part, left_side, preferred_element_type=...  14.2 us
  transfers between devices with their start and end apart: 7, of which 6 were waited for; matrix products, arithmetic and copies ran while one was open for 5% of the time, Pallas kernels for 0%

profile of v1, /device:TPU:0, one launch (start us, length us, event | category | flops | bytes accessed | tf_op | source)
XLA Modules:
  0.0 613.5 jit_solution(15077956494862034796)
XLA Ops:
  7.2 0.0 all-gather.2.cloned.1.call-start
  7.3 3.5 convert_reduce_fusion
  10.8 4.8 fusion.10
  15.6 0.1 fusion.45
  15.7 0.1 broadcast_multiply_fusion.1
  15.8 8.7 %convolution_bitcast_fusion = f32[4,128,64,128]{3,2,0,1:T(8,128)S(1)} fusion(bf16[128,128,128]{2,1,0:T(8,128)(2,1)} %param.5, f32[128]{0:T(128)S(1)} %copy-done.12, f32[128,128]{1,0:T(8,128)S(1)} %add_rsqrt_fusion, f32[128,128]{1,0:T(8,128)S(1)} %broadcast_multiply_fusion.4, bf16[4,128,64]{1,2,0:T(8,128)(2,1)S(1)} %copy-done), kind=kOutput, calls=%fused_computation.7 | convolution fusion | flops 1084227584 | bytes 21168640 | tf_op jit(solution)/shard_map/ikd,wdc->wick/dot_general | solution.py:29
  24.6 5.7 copy-done.1
  30.3 2.6 multiply_convert_fusion.5
  32.9 0.0 all-gather.2.cloned.1.call-update
  32.9 0.0 reduce-scatter.2.cloned.1.call-start
  33.0 1.4 copy.20
  34.3 3.1 collective-permute-start
  37.4 47.6 %collective-permute-done = bf16[128,64,128]{2,0,1:T(8,128)(2,1)S(1)} collective-permute-done((bf16[128,64,128]{2,0,1:T(8,128)(2,1)S(1)}, bf16[128,64,128]{2,0,1:T(8,128)(2,1)S(1)}, u32[]{:S(2)}, u32[]{:S(2)}) %collective-permute-start) | collective-permute-done | bytes 2097184 | tf_op jit(solution)/shard_map/ppermute | solution.py:34
  85.1 1.3 copy-done.7
  86.4 48.7 %collective-permute-done.1 = bf16[128,64,128]{2,0,1:T(8,128)(2,1)} collective-permute-done((bf16[128,64,128]{2,0,1:T(8,128)(2,1)S(1)}, bf16[128,64,128]{2,0,1:T(8,128)(2,1)}, u32[]{:S(2)}, u32[]{:S(2)}) %collective-permute-start.1) | collective-permute-done | bytes 2097184 | tf_op jit(solution)/shard_map/ppermute | solution.py:34
  135.1 0.5 collective-permute-start.2
  135.6 48.0 %collective-permute-done.2 = bf16[128,64,128]{2,0,1:T(8,128)(2,1)} collective-permute-done((bf16[128,64,128]{2,0,1:T(8,128)(2,1)}, bf16[128,64,128]{2,0,1:T(8,128)(2,1)}, u32[]{:S(2)}, u32[]{:S(2)}) %collective-permute-start.2) | collective-permute-done | bytes 2097184 | tf_op jit(solution)/shard_map/ppermute | solution.py:34
  183.6 3.4 constant_dynamic-update-slice_fusion.7
  187.0 3.3 constant_dynamic-update-slice_fusion.6
  190.2 1.6 constant_dynamic-update-slice_fusion.5
  191.8 2.9 constant_dynamic-update-slice_fusion.4
  194.7 3.3 constant_dynamic-update-slice_fusion.3
  198.1 3.4 constant_dynamic-update-slice_fusion.2
  201.5 1.6 constant_dynamic-update-slice_fusion.1
  203.1 2.8 constant_dynamic-update-slice_fusion
  205.9 25.2 %fusion.11 = f32[64,128,128]{2,1,0:T(8,128)} fusion(bf16[512,64,128]{2,1,0:T(8,128)(2,1)} %all-gather.2.cloned.1.call-done, bf16[128,64,1024]{2,0,1:T(8,128)(2,1)} %constant_dynamic-update-slice_fusion, s32[]{:T(128)S(6)} %select_n.22), kind=kOutput, calls=%fused_computation.15 | convolution fusion | flops 1073741824 | bytes 20971524 | tf_op jit(solution)/shard_map/icj,jck->ick/dot_general | solution.py:39
  231.1 5.6 copy.24
  236.7 7.0 %fusion.31 = (bf16[1,128,64,128]{3,2,1,0:T(8,128)(2,1)S(1)}, bf16[1,128,64,128]{3,2,1,0:T(8,128)(2,1)}, bf16[128,64,128]{2,1,0:T(8,128)(2,1)S(1)}) fusion(f32[64,128,128]{1,0,2:T(8,128)} %copy.24, f32[128,128]{1,0:T(8,128)S(1)} %broadcast_multiply_fusion.1, f32[4,128,64,128]{3,2,0,1:T(8,128)} %copy-done.1), kind=kLoop, calls=%fused_computation.46 | loop fusion | flops 14680064 | bytes 18939904 | tf_op jit(solution)/shard_map/stack | solution.py:54
  243.7 14.2 %fusion.13 = f32[64,128,512]{2,1,0:T(8,128)} fusion(bf16[128,64,1024]{2,0,1:T(8,128)(2,1)} %constant_dynamic-update-slice_fusion, s32[]{:T(128)S(6)} %select_n.22, bf16[128,64,128]{2,1,0:T(8,128)(2,1)S(1)} %get-tuple-element.8), kind=kOutput, calls=%fused_computation.18 | convolution fusion | flops 1073741824 | bytes 27262980 | tf_op jit(solution)/shard_map/icj,ick->jck/dot_general | solution.py:47
  257.9 16.6 %copy.27 = f32[64,128,512]{1,0,2:T(8,128)} copy(f32[64,128,512]{2,1,0:T(8,128)} %fusion.13) | data formatting | bytes 33554432 | tf_op jit(solution)/shard_map/icj,ick->jck/dot_general | solution.py:47
  274.4 0.0 reduce-scatter.2.cloned.1.call-update
  274.4 0.0 all-reduce.5.cloned.1.call-start
  274.5 151.6 %reduce-scatter.2.cloned.1.call-done = f32[128,64,128]{2,1,0:T(8,128)} async-done(((f32[512,64,128]{2,1,0:T(8,128)}), f32[128,64,128]{2,1,0:T(8,128)}) %reduce-scatter.2.cloned.1.call-update) | async-done | bytes 4194320 | tf_op jit(solution)/shard_map/reduce_scatter | solution.py:46
  426.1 6.1 fusion.33
  432.2 1.3 copy-done.10
  433.6 0.6 copy-done.11
  434.2 5.4 fusion.36
  439.6 0.0 all-reduce.5.cloned.1.call-update
  439.7 0.0 all-reduce.3.cloned.1.call-start
  439.7 6.5 %convolution_bitcast_fusion.1 = f32[128,128,128]{2,1,0:T(8,128)} fusion(bf16[1,128,64,128]{3,2,1,0:T(8,128)(2,1)} %copy-done.11, bf16[1,128,64,128]{3,2,1,0:T(8,128)(2,1)} %copy-done.10, bf16[1,128,64,128]{3,2,1,0:T(8,128)(2,1)} %get-tuple-element.5, bf16[1,128,64,128]{3,2,1,0:T(8,128)(2,1)S(1)} %get-tuple-element.4, bf16[4,128,64]{1,2,0:T(8,128)(2,1)S(1)} %copy-done), kind=kOutput, calls=%fused_computation.45 | convolution fusion | flops 1086324736 | bytes 16842752 | tf_op jit(solution)/shard_map/wick,wdc->ikd/dot_general | solution.py:56
  446.2 0.0 all-reduce.3.cloned.1.call-update
  446.3 98.9 %all-reduce.5.cloned.1.call-done = f32[4,128,64]{1,2,0:T(8,128)} async-done(((f32[4,128,64]{1,2,0:T(8,128)}), f32[4,128,64]{1,2,0:T(8,128)}) %all-reduce.5.cloned.1.call-update) | async-done | bytes 131088 | tf_op jit(solution)/shard_map/psum | solution.py:66
  545.2 1.5 multiply_reduce_fusion.1
  546.8 3.1 psum.23
  550.5 1.6 broadcast_multiply_fusion
  552.1 32.2 %all-reduce.3.cloned.1.call-done = f32[128,128,128]{2,1,0:T(8,128)} async-done(((f32[128,128,128]{2,1,0:T(8,128)}), f32[128,128,128]{2,1,0:T(8,128)}) %all-reduce.3.cloned.1.call-update) | async-done | bytes 8388624 | tf_op jit(solution)/shard_map/psum | solution.py:59
  584.3 11.6 %multiply_reduce_fusion = (f32[128,128]{1,0:T(8,128)S(1)}, f32[128,128]{1,0:T(8,128)S(1)}) fusion(f32[128,128,128]{2,1,0:T(8,128)} %all-reduce.3.cloned.1.call-done, f32[128]{0:T(128)S(1)} %copy-done.12, f32[128,128]{1,0:T(8,128)S(1)} %add_rsqrt_fusion, f32[128,128]{1,0:T(8,128)S(1)} %broadcast_multiply_fusion.4, bf16[128,128,128]{2,1,0:T(8,128)(2,1)} %param.5), kind=kLoop, calls=%fused_computation.17 | loop fusion | flops 14647296 | bytes 12845568 | tf_op jit(solution)/shard_map/reduce_sum | solution.py:63
  595.9 10.7 %fusion.9 = bf16[128,128,128]{2,1,0:T(8,128)(2,1)} fusion(bf16[128,128,128]{2,1,0:T(8,128)(2,1)S(1)} %copy-done.4, f32[128,128,128]{2,1,0:T(8,128)S(1)} %copy-done.5, f32[128,128]{1,0:T(8,128)S(1)} %get-tuple-element.11, f32[128,128]{1,0:T(8,128)S(1)} %get-tuple-element.12, f32[128]{0:T(128)S(1)} %copy-done.12, f32[128,128]{1,0:T(8,128)S(1)} %add_rsqrt_fusion, ...), kind=kLoop, calls=%fused_computation.12 | loop fusion | flops 18874368 | bytes 17039872 | tf_op jit(solution)/shard_map/convert_element_type | solution.py:70
  (30 shorter events, 0.1 us)
Async XLA Ops:
  7.2 8.6 %copy-start = (bf16[4,128,64]{1,2,0:T(8,128)(2,1)S(1)}, bf16[4,128,64]{1,2,0:T(8,128)(2,1)}, u32[]{:S(2)}) copy-start(bf16[4,128,64]{1,2,0:T(8,128)(2,1)} %param.7) | copy-start | bytes 196612
  7.2 198.7 %all-gather.2.cloned.1.call-start = ((), (), s32[]{:S(2)}) async-start(), calls=%async_computation.1 | async-start | bytes 10485760 | tf_op jit(solution)/shard_map/all_gather | solution.py:42
  7.2 3.6 copy-start.2
  7.2 8.4 %copy-start.13 = (s32[512]{0:T(512)S(1)}, s32[512]{0:T(512)}, u32[]{:S(2)}) copy-start(s32[512]{0:T(512)} %param.8) | copy-start | bytes 6148
  7.3 8.6 %copy-start.12 = (f32[128]{0:T(128)S(1)}, f32[128]{0:T(128)}, u32[]{:S(2)}) copy-start(f32[128]{0:T(128)} %param.6) | copy-start | bytes 1540
  24.5 5.7 copy-start.1
  30.3 2.7 copy-start.6
  32.9 393.2 %reduce-scatter.2.cloned.1.call-start = ((), (), s32[]{:S(2)}) async-start(), calls=%async_computation.2 | async-start | bytes 20971520 | tf_op jit(solution)/shard_map/reduce_scatter | solution.py:46
  34.3 50.8 %collective-permute-start = (bf16[128,64,128]{2,0,1:T(8,128)(2,1)S(1)}, bf16[128,64,128]{2,0,1:T(8,128)(2,1)S(1)}, u32[]{:S(2)}, u32[]{:S(2)}) collective-permute-start(bf16[128,64,128]{2,0,1:T(8,128)(2,1)S(1)} %copy.20), channel_id=1, source_target_pairs={{0,2},{2,4},{4,6},{6,0},{1,3},{3,5},{5,7},{7,1},{8,10},{10,12},{12... | collective-permute-start | bytes 6291464 | tf_op jit(solution)/shard_map/ppermute | solution.py:34
  85.1 1.3 copy-start.7
  86.4 48.7 %collective-permute-start.1 = (bf16[128,64,128]{2,0,1:T(8,128)(2,1)S(1)}, bf16[128,64,128]{2,0,1:T(8,128)(2,1)}, u32[]{:S(2)}, u32[]{:S(2)}) collective-permute-start(bf16[128,64,128]{2,0,1:T(8,128)(2,1)S(1)} %collective-permute-done), channel_id=1, source_target_pairs={{0,2},{2,4},{4,6},{6,0},{1,3},{3,5},{5,7},{7,1},{8,10},{10,12},{12... | collective-permute-start | bytes 6291464 | tf_op jit(solution)/shard_map/ppermute | solution.py:34
  135.1 48.5 %collective-permute-start.2 = (bf16[128,64,128]{2,0,1:T(8,128)(2,1)}, bf16[128,64,128]{2,0,1:T(8,128)(2,1)}, u32[]{:S(2)}, u32[]{:S(2)}) collective-permute-start(bf16[128,64,128]{2,0,1:T(8,128)(2,1)} %collective-permute-done.1), channel_id=1, source_target_pairs={{0,2},{2,4},{4,6},{6,0},{1,3},{3,5},{5,7},{7,1},{8,10},{10,12},{12... | collective-permute-start | bytes 6291464 | tf_op jit(solution)/shard_map/ppermute | solution.py:34
  135.6 54.7 %copy-start.8 = (bf16[128,64,128]{2,0,1:T(8,128)(2,1)S(1)}, bf16[128,64,128]{2,0,1:T(8,128)(2,1)}, u32[]{:S(2)}) copy-start(bf16[128,64,128]{2,0,1:T(8,128)(2,1)} %copy-done.7) | copy-start | bytes 6291460
  274.4 270.8 %all-reduce.5.cloned.1.call-start = ((), (), s32[]{:S(2)}) async-start(), calls=%async_computation.4 | async-start | bytes 262144 | tf_op jit(solution)/shard_map/psum | solution.py:66
  426.1 8.1 %copy-start.3 = (bf16[128,128,128]{2,1,0:T(8,128)(2,1)S(1)}, bf16[128,128,128]{2,1,0:T(8,128)(2,1)}, u32[]{:S(2)}) copy-start(bf16[128,128,128]{2,1,0:T(8,128)(2,1)} %param.5) | copy-start | bytes 12582916
  426.1 8.1 %copy-start.9 = (bf16[1,128,64,128]{3,2,1,0:T(8,128)(2,1)S(1)}, bf16[1,128,64,128]{3,2,1,0:T(8,128)(2,1)}, u32[]{:S(2)}) copy-start(bf16[1,128,64,128]{3,2,1,0:T(8,128)(2,1)} %get-tuple-element.5) | copy-start | bytes 6291460
  432.2 1.3 copy-start.10
  432.2 2.0 copy-start.11
  439.7 144.6 %all-reduce.3.cloned.1.call-start = ((), (), s32[]{:S(2)}) async-start(), calls=%async_computation.3 | async-start | bytes 16777216 | tf_op jit(solution)/shard_map/psum | solution.py:59
  584.3 11.6 %copy-start.4 = (bf16[128,128,128]{2,1,0:T(8,128)(2,1)S(1)}, bf16[128,128,128]{2,1,0:T(8,128)(2,1)}, u32[]{:S(2)}) copy-start(bf16[128,128,128]{2,1,0:T(8,128)(2,1)} %param.5) | copy-start | bytes 12582916
  584.3 11.6 %copy-start.5 = (f32[128,128,128]{2,1,0:T(8,128)S(1)}, f32[128,128,128]{2,1,0:T(8,128)}, u32[]{:S(2)}) copy-start(f32[128,128,128]{2,1,0:T(8,128)} %all-reduce.3.cloned.1.call-done) | copy-start | bytes 25165828
Sparse Core Ops, SparseCore 0:
  33.0 90.1 all-gather.1
  274.6 151.5 reduce-scatter.1
  439.8 105.3 all-reduce.4
  547.5 36.6 all-reduce.2
